TPU v7x, 256 devices: a whole 4x4x8 slice. The times are simulated.
256 devices in a mesh: shadow: 32 (over z, y_lo, core), vocab: 8 (over y_hi, x).
Axes of the slice: x: 4, y: 4 (y_hi: 2, y_lo: 2; y = y_hi * 2 + y_lo), z: 8, core: 2. Of those that a mesh axis runs over, the one named last changes fastest.
Arguments:
- hidden: bfloat16 [128, 128, 2048], P('shadow'), may hold values from -18 to 18
- targets: int32 [128], replicated, may hold values from 0 to 32767
- membership: int32 [128, 4], P('shadow'), may hold values from 0 to 1, as said below
- unembedding: bfloat16 [32768, 2048], P(('shadow', 'vocab')), may hold values from -1 to 1
Outputs:
- score: float32 [128, 128], P('shadow', 'vocab')
Inputs may be any that keep to these rules, and one draw needn't show every extreme that they name: `membership`: each candidate sequence is a member of exactly 64 of the shadow models.
All inputs are finite; a program needn't handle non-finite values.
Results may differ from a plain program's by a relative error of at most 0.00055.
Values may be sent and summed in bfloat16 or wider, within the bound.
No kernel may reach another device: no remote copies, remote signals or barrier semaphores. Data moves between devices by JAX's collectives and lax.ppermute only.
A program may use at most 64 MiB of HBM per device.

v0:
```python
import jax
import jax.numpy as jnp
from jax import lax
from jax.sharding import PartitionSpec as P

SEQ = 32
NEG_FILL = -1e30
VAR_FLOOR = 0.5


def copy_for_each(value, axis):
    copies = jnp.broadcast_to(value, (lax.axis_size(axis), *value.shape))
    return lax.all_to_all(copies, axis, split_axis=0, concat_axis=0, tiled=True)


def all_in_one(value, axis):
    leaves = jax.tree.leaves(value)
    sequence = sorted(range(len(leaves)), key=lambda k: -leaves[k].size)
    width = (1, *leaves[sequence[0]].shape)[-1]
    lines = [
        jnp.pad(leaves[k].reshape(-1), (0, -leaves[k].size % width)).reshape(-1, width)
        for k in sequence
    ]
    both, at, found = (copy_for_each(jnp.concatenate(lines), axis), 0, {})
    for k, line in zip(sequence, lines):
        share = both[:, at : at + len(line)].reshape(len(both), -1)
        found[k] = share[:, : leaves[k].size].reshape(-1, *leaves[k].shape)
        at += len(line)
    numbers = iter(range(len(leaves)))
    return jax.tree.map(lambda _: found[next(numbers)], value)


def folded_in_pairs(pieces, combine):
    while len(jax.tree.leaves(pieces)[0]) > 1:
        pieces = jax.vmap(combine)(
            *(jax.tree.map(lambda part: part[side::2], pieces) for side in (0, 1))
        )
    return jax.tree.map(lambda part: part[0], pieces)


def joined_all(value, axis, combine):
    pieces = all_in_one(value, axis)
    return folded_in_pairs(pieces, combine)


def over_copies(value, axis):
    everything = copy_for_each(value, axis)
    return jnp.sum(everything, axis=0)


def packed_total(arrays, axis):
    ends = [0]
    for a in arrays:
        ends.append(ends[-1] + a.size)
    total = over_copies(jnp.concatenate([a.ravel() for a in arrays]), axis)
    return tuple((total[b:e].reshape(a.shape) for a, b, e in zip(arrays, ends, ends[1:])))


def start_state(row_count):
    return (
        jnp.full((row_count,), NEG_FILL, jnp.float32),
        jnp.zeros((row_count,), jnp.float32),
        jnp.zeros((row_count,), jnp.float32),
    )


def fold_block(running, flat_rows, wanted, block_rows, vocab_rows):
    highest, summed, target_logit = running
    logits = lax.dot_general(
        flat_rows, block_rows, (((1,), (1,)), ((), ())), preferred_element_type=jnp.float32
    )
    target_hit = wanted[:, None] == vocab_rows[None, :]
    target_logit = jnp.sum(jnp.where(target_hit, logits, 0.0), axis=1)
    others = jnp.where(target_hit, NEG_FILL, logits)
    raised = jnp.maximum(highest, jnp.max(others, axis=1))
    fresh_terms = jnp.where(target_hit, 0.0, jnp.exp(others - raised[:, None]))
    summed = jnp.sum(fresh_terms, axis=1)
    return (raised, summed, target_logit)


def combine_pairs(earlier, latter):
    raised = jnp.maximum(earlier[0], latter[0])
    summed = earlier[1] * jnp.exp(earlier[0] - raised) + latter[1] * jnp.exp(latter[0] - raised)
    return (raised, summed, earlier[2] + latter[2])


def per_device(hidden, targets, membership, unembedding):
    shadow_count, token_count, model_width = hidden.shape
    head_rows = unembedding.shape[0]
    vocab_count = lax.axis_size("vocab")
    vocab_index = lax.axis_index("vocab")
    shadows_total = shadow_count * lax.axis_size("shadow")
    slice_tokens = token_count // vocab_count
    slice_start = vocab_index * slice_tokens
    flat_rows = hidden.reshape(shadow_count * token_count, model_width)
    wanted = jnp.tile(targets, shadow_count)
    block_rows = lax.all_gather(unembedding, "shadow", axis=0, tiled=True)
    gathered = jnp.arange(block_rows.shape[0], dtype=jnp.int32)
    vocab_rows = (
        gathered // head_rows * vocab_count + vocab_index
    ) * head_rows + gathered % head_rows
    highest, summed, target_logit = fold_block(
        start_state(flat_rows.shape[0]), flat_rows, wanted, block_rows, vocab_rows
    )
    highest, summed, target_logit = joined_all(
        (highest, summed, target_logit), "vocab", combine_pairs
    )
    all_confidence = (target_logit - (highest + jnp.log(summed))).reshape(shadow_count, token_count)
    confidence = lax.dynamic_slice_in_dim(all_confidence, slice_start, slice_tokens, 1)
    member_tokens = jnp.repeat(membership, SEQ, axis=1)
    outside = (1 - lax.dynamic_slice_in_dim(member_tokens, slice_start, slice_tokens, 1)).astype(
        jnp.float32
    )
    weighted = outside * confidence
    first_moment, second_moment = packed_total(
        (jnp.sum(weighted, axis=0), jnp.sum(weighted * confidence, axis=0)), "shadow"
    )
    out_count = shadows_total // 2 - outside
    out_mean = (first_moment[None, :] - weighted) / out_count
    out_variance = (
        second_moment[None, :] - weighted * confidence
    ) / out_count - out_mean * out_mean
    return (confidence - out_mean) * lax.rsqrt(jnp.maximum(out_variance, 0.0) + VAR_FLOOR)


def solution(mesh):
    return jax.shard_map(
        per_device,
        mesh=mesh,
        in_specs=(P("shadow", None, None), P(), P("shadow", None), P(("shadow", "vocab"), None)),
        out_specs=P("shadow", "vocab"),
        check_vma=False,
    )
```

profile of v0, /device:TPU:1, one launch (start us, length us, event | category | flops | bytes accessed | tf_op | source)
XLA Modules:
  0.0 166.2 jit_solution(9505137555500328018)
XLA Ops:
  6.5 0.0 copy-start
  6.5 0.0 all-gather.2.cloned.1.call-start
  6.5 0.7 all-gather.2.cloned.1.call-update
  7.3 0.7 broadcast_bitcast_fusion
  7.9 105.2 %all-gather.2.cloned.1.call-done = bf16[4096,2048]{1,0:T(8,128)(2,1)} async-done(((bf16[128,2048]{1,0:T(8,128)(2,1)}), bf16[4096,2048]{1,0:T(8,128)(2,1)}) %all-gather.2.cloned.1.call-update) | async-done | bytes 16777232 | tf_op jit(solution)/shard_map/all_gather | solution.py:97
  113.1 0.0 copy-done
  113.1 12.0 %fusion.2 = (f32[512]{0:T(512)S(1)}, f32[512,4096]{1,0:T(8,128)S(1)}) fusion(s32[4096]{0:T(1024)S(1)} %fusion.12, s32[512]{0:T(512)S(1)} %broadcast_bitcast_fusion, bf16[512,2048]{1,0:T(8,128)(2,1)S(1)} %bitcast.17, bf16[4096,2048]{1,0:T(8,128)(2,1)} %all-gather.2.cloned.1.call-done), kind=kOutput, calls=%fused_computation.5 | convolution fusion | flops 8596226048 | bytes 27283456 | tf_op jit(solution)/shard_map/dot_general | solution.py:69
  125.1 0.0 copy-start.1
  125.2 3.4 %fusion = (f32[512]{0:T(512)S(1)}, f32[512]{0:T(512)S(1)}) fusion(f32[512,4096]{1,0:T(8,128)S(1)} %get-tuple-element.19, f32[512]{0:T(512)S(1)} %broadcast_maximum_fusion, s32[4096]{0:T(1024)S(1)} %fusion.12, s32[512]{0:T(512)S(1)} %broadcast_bitcast_fusion), kind=kLoop, calls=%fused_computation.3 | loop fusion | flops 14679040 | bytes 8413184 | tf_op jit(solution)/shard_map/reduce_sum | solution.py:77
  128.6 0.6 broadcast_in_dim.28
  129.2 6.4 %all-to-all-start = ((f32[8,3,512]{2,1,0:T(4,128)}), f32[8,3,512]{2,1,0:T(4,128)S(1)}, u32[]{:S(2)}, u32[]{:S(2)}) async-start(f32[8,3,512]{2,1,0:T(4,128)} %broadcast_in_dim.28), calls=%async_computation | async-start | bytes 131072 | tf_op jit(solution)/shard_map/all_to_all | solution.py:13
  135.6 0.0 copy-done.1
  135.7 0.1 broadcast_in_dim.29
  135.7 0.1 reshape.79
  135.8 6.5 %all-to-all-done = f32[8,3,512]{2,1,0:T(4,128)S(1)} async-done(((f32[8,3,512]{2,1,0:T(4,128)}), f32[8,3,512]{2,1,0:T(4,128)S(1)}, u32[]{:S(2)}, u32[]{:S(2)}) %all-to-all-start) | async-done | bytes 49184 | tf_op jit(solution)/shard_map/all_to_all | solution.py:13
  142.8 0.1 fusion.17
  142.9 0.1 pad_maximum_fusion.1
  143.0 15.7 %all_to_all.11 = f32[32,1,32]{2,1,0:T(1,128)S(1)} all-to-all(f32[32,1,32]{2,1,0:T(1,128)S(1)} %broadcast_in_dim.30), channel_id=1, replica_groups=mesh['shadow'=32,'vocab'=8] {'shadow'}, dimensions={0} | all-to-all | bytes 8192 | tf_op jit(solution)/shard_map/all_to_all | solution.py:13
  158.6 0.1 fusion.21
  158.7 0.7 rsqrt_multiply_fusion
  (25 shorter events, 0.5 us)
Async XLA Ops:
  6.5 106.6 %copy-start = (bf16[4,128,2048]{2,1,0:T(8,128)(2,1)S(1)}, bf16[4,128,2048]{2,1,0:T(8,128)(2,1)}, u32[]{:S(2)}) copy-start(bf16[4,128,2048]{2,1,0:T(8,128)(2,1)} %param.4) | copy-start | bytes 6291460
  6.5 106.6 %all-gather.2.cloned.1.call-start = ((), (), s32[]{:S(2)}) async-start(), calls=%async_computation.2 | async-start | bytes 17301504 | tf_op jit(solution)/shard_map/all_gather | solution.py:97
  125.1 10.5 %copy-start.1 = (s32[4,4]{1,0:T(4,128)S(1)}, s32[4,4]{1,0:T(4,128)}, u32[]{:S(2)}) copy-start(s32[4,4]{1,0:T(4,128)} %param.6) | copy-start | bytes 196
  129.2 13.1 %all-to-all-start = ((f32[8,3,512]{2,1,0:T(4,128)}), f32[8,3,512]{2,1,0:T(4,128)S(1)}, u32[]{:S(2)}, u32[]{:S(2)}) async-start(f32[8,3,512]{2,1,0:T(4,128)} %broadcast_in_dim.28), calls=%async_computation | async-start | bytes 131072 | tf_op jit(solution)/shard_map/all_to_all | solution.py:13
Sparse Core Ops, SparseCore 0:
  9.2 103.8 all-gather.1
where the time goes:
time: 166 us
  waiting for transfers between devices  112 us (67%)
  blocking collectives  15.7 us (9%)
  between operations  13.5 us (8%)
  matrix products  12 us (7%)
  starting transfers between devices  6.42 us (4%)
  other arithmetic  4.39 us (3%)
  local copies, waits for them, and re-layouts  1.87 us (1%)
    all_gather x1, waiting for transfers between devices, per_device(): block_rows = lax.all_gather(unembedding, 'shadow', axis=0, tiled=True)  105 us
    all_to_all x1, blocking collectives, copy_for_each(): return lax.all_to_all(copies, axis, split_axis=0, concat_axis=0, tiled=True)  15.7 us
    dot_general x1, matrix products, fold_block(): lax.dot_general(flat_rows, block_rows, (((1,), (1,)), ((), ())), preferre...  12 us
    all_to_all x1, waiting for transfers between devices, copy_for_each(): return lax.all_to_all(copies, axis, split_axis=0, concat_axis=0, tiled=True)  6.54 us
    all_to_all x1, starting transfers between devices, copy_for_each(): return lax.all_to_all(copies, axis, split_axis=0, concat_axis=0, tiled=True)  6.42 us
    reduce_sum x1, other arithmetic, fold_block(): summed = jnp.sum(fresh_terms, axis=1)  3.42 us
  transfers between devices with their start and end apart: 2, of which 2 were waited for; matrix products, arithmetic and copies ran while one was open for 0% of the time, Pallas kernels for 0%

commit v1 on v0

--- a/solution.py
+++ b/solution.py
@@ -94,7 +94,10 @@
     slice_start = vocab_index * slice_tokens
     flat_rows = hidden.reshape(shadow_count * token_count, model_width)
     wanted = jnp.tile(targets, shadow_count)
-    block_rows = lax.all_gather(unembedding, "shadow", axis=0, tiled=True)
+    value_now = lax.axis_size("shadow")
+    response = jnp.stack(value_now * [unembedding], axis=0)
+    mat_out = lax.all_to_all(response, axis_name="shadow", split_axis=0, concat_axis=0)
+    block_rows = jnp.concatenate(mat_out, 0)
     gathered = jnp.arange(block_rows.shape[0], dtype=jnp.int32)
     vocab_rows = (
         gathered // head_rows * vocab_count + vocab_index

time: 166 us -> 428 us (2.58)
  waiting for transfers between devices: 112 us -> 365 us
  between operations: 13.5 us -> 0.11 us
  starting transfers between devices: 6.42 us -> 17.7 us
  local copies, waits for them, and re-layouts: 1.87 us -> 8.15 us
  blocking collectives: 15.7 us -> 20.7 us
    all_to_all x0 -> x1, waiting for transfers between devices: none -> 359 us  [per_device(): lax.all_to_all(response, axis_name='shadow', split_axis=0, concat_axis=0)]
    all_gather x1 -> x0, waiting for transfers between devices: 105 us -> none  [per_device(): block_rows = lax.all_gather(unembedding, 'shadow', axis=0, tiled=True)]
    all_to_all x0 -> x1, starting transfers between devices: none -> 11.3 us  [per_device(): lax.all_to_all(response, axis_name='shadow', split_axis=0, concat_axis=0)]
    another operation x0 -> x1, local copies, waits for them, and re-layouts: none -> 6.94 us  [per_device(): response = jnp.stack(value_now * [unembedding], axis=0)]
    all_to_all x1, blocking collectives: 15.7 us -> 20.7 us  [copy_for_each(): return lax.all_to_all(copies, axis, split_axis=0, concat_axis=0, tiled=True)]
where the time goes in v1:
time: 428 us
  waiting for transfers between devices  365 us (85%)
  blocking collectives  20.7 us (5%)
  starting transfers between devices  17.7 us (4%)
  matrix products  12 us (3%)
  local copies, waits for them, and re-layouts  8.15 us (2%)
  other arithmetic  4.39 us (1%)
    all_to_all x1, waiting for transfers between devices, per_device(): lax.all_to_all(response, axis_name='shadow', split_axis=0, concat_axis=0)  359 us
    all_to_all x1, blocking collectives, copy_for_each(): return lax.all_to_all(copies, axis, split_axis=0, concat_axis=0, tiled=True)  20.7 us
    dot_general x1, matrix products, fold_block(): lax.dot_general(flat_rows, block_rows, (((1,), (1,)), ((), ())), preferre...  12 us
    all_to_all x1, starting transfers between devices, per_device(): lax.all_to_all(response, axis_name='shadow', split_axis=0, concat_axis=0)  11.3 us
  transfers between devices with their start and end apart: 2, of which 2 were waited for; matrix products, arithmetic and copies ran while one was open for 0% of the time, Pallas kernels for 0%

profile of v1, /device:TPU:1, one launch (start us, length us, event | category | flops | bytes accessed | tf_op | source)
XLA Modules:
  0.0 428.1 jit_solution(16186461959116896156)
XLA Ops:
  0.0 0.0 copy-start
  0.0 6.9 %stack.2 = bf16[32,128,2048]{2,1,0:T(8,128)(2,1)} broadcast(bf16[128,2048]{1,0:T(8,128)(2,1)} %param.7), dimensions={1,2} | broadcast | bytes 17301504 | tf_op jit(solution)/shard_map/stack | solution.py:98
  6.9 0.0 copy-start.2
  6.9 11.3 %all-to-all-start = ((bf16[32,128,2048]{2,1,0:T(8,128)(2,1)}), bf16[32,128,2048]{2,1,0:T(8,128)(2,1)}, u32[]{:S(2)}, u32[]{:S(2)}) async-start(bf16[32,128,2048]{2,1,0:T(8,128)(2,1)} %stack.2), calls=%async_computation | async-start | bytes 33554432 | tf_op jit(solution)/shard_map/all_to_all | solution.py:99
  18.3 0.0 copy-done.2
  18.3 358.5 %all-to-all-done = bf16[32,128,2048]{2,1,0:T(8,128)(2,1)} async-done(((bf16[32,128,2048]{2,1,0:T(8,128)(2,1)}), bf16[32,128,2048]{2,1,0:T(8,128)(2,1)}, u32[]{:S(2)}, u32[]{:S(2)}) %all-to-all-start) | async-done | bytes 16777248 | tf_op jit(solution)/shard_map/all_to_all | solution.py:99
  376.8 0.0 copy-done
  376.8 12.0 %fusion.2 = (f32[512]{0:T(512)S(1)}, f32[512,4096]{1,0:T(8,128)S(1)}) fusion(s32[4096]{0:T(1024)S(1)} %fusion.12, s32[512]{0:T(512)S(1)} %broadcast_bitcast_fusion, bf16[512,2048]{1,0:T(8,128)(2,1)S(1)} %bitcast.18, bf16[4096,2048]{1,0:T(8,128)(2,1)} %bitcast.2), kind=kOutput, calls=%fused_computation.5 | convolution fusion | flops 8596226048 | bytes 27283456 | tf_op jit(solution)/shard_map/dot_general | solution.py:69
  388.9 0.0 copy-start.1
  388.9 3.4 fusion
  392.3 0.6 broadcast_in_dim.28
  393.0 6.4 %all-to-all-start.1 = ((f32[8,3,512]{2,1,0:T(4,128)}), f32[8,3,512]{2,1,0:T(4,128)S(1)}, u32[]{:S(2)}, u32[]{:S(2)}) async-start(f32[8,3,512]{2,1,0:T(4,128)} %broadcast_in_dim.28), calls=%async_computation.1 | async-start | bytes 131072 | tf_op jit(solution)/shard_map/all_to_all | solution.py:13
  399.3 0.0 copy-done.1
  399.3 0.1 broadcast_in_dim.29
  399.4 0.1 reshape.85
  399.5 6.5 %all-to-all-done.1 = f32[8,3,512]{2,1,0:T(4,128)S(1)} async-done(((f32[8,3,512]{2,1,0:T(4,128)}), f32[8,3,512]{2,1,0:T(4,128)S(1)}, u32[]{:S(2)}, u32[]{:S(2)}) %all-to-all-start.1) | async-done | bytes 49184 | tf_op jit(solution)/shard_map/all_to_all | solution.py:13
  406.5 0.1 fusion.17
  406.6 0.1 pad_maximum_fusion.1
  406.6 20.7 %all_to_all.16 = f32[32,1,32]{2,1,0:T(1,128)S(1)} all-to-all(f32[32,1,32]{2,1,0:T(1,128)S(1)} %broadcast_in_dim.30), channel_id=1, replica_groups=mesh['shadow'=32,'vocab'=8] {'shadow'}, dimensions={0} | all-to-all | bytes 8192 | tf_op jit(solution)/shard_map/all_to_all | solution.py:13
  427.4 0.1 fusion.21
  427.5 0.7 rsqrt_multiply_fusion
  (26 shorter events, 0.5 us)
Async XLA Ops:
  0.0 376.8 %copy-start = (bf16[4,128,2048]{2,1,0:T(8,128)(2,1)S(1)}, bf16[4,128,2048]{2,1,0:T(8,128)(2,1)}, u32[]{:S(2)}) copy-start(bf16[4,128,2048]{2,1,0:T(8,128)(2,1)} %param.4) | copy-start | bytes 6291460
  6.9 11.3 %copy-start.2 = (s32[128]{0:T(128)S(1)}, s32[128]{0:T(128)}, u32[]{:S(2)}) copy-start(s32[128]{0:T(128)} %param.5) | copy-start | bytes 1540
  6.9 369.9 %all-to-all-start = ((bf16[32,128,2048]{2,1,0:T(8,128)(2,1)}), bf16[32,128,2048]{2,1,0:T(8,128)(2,1)}, u32[]{:S(2)}, u32[]{:S(2)}) async-start(bf16[32,128,2048]{2,1,0:T(8,128)(2,1)} %stack.2), calls=%async_computation | async-start | bytes 33554432 | tf_op jit(solution)/shard_map/all_to_all | solution.py:99
  388.9 10.5 %copy-start.1 = (s32[4,4]{1,0:T(4,128)S(1)}, s32[4,4]{1,0:T(4,128)}, u32[]{:S(2)}) copy-start(s32[4,4]{1,0:T(4,128)} %param.6) | copy-start | bytes 196
  393.0 13.1 %all-to-all-start.1 = ((f32[8,3,512]{2,1,0:T(4,128)}), f32[8,3,512]{2,1,0:T(4,128)S(1)}, u32[]{:S(2)}, u32[]{:S(2)}) async-start(f32[8,3,512]{2,1,0:T(4,128)} %broadcast_in_dim.28), calls=%async_computation.1 | async-start | bytes 131072 | tf_op jit(solution)/shard_map/all_to_all | solution.py:13
